TPU v7x, 32 devices: a whole 2x2x4 slice. The times are simulated.
32 devices in a mesh: amp: 32 (over z, y, x, core).
Axes of the slice: x: 2, y: 2, z: 4, core: 2. Of those that a mesh axis runs over, the one named last changes fastest.
Arguments:
- ket_state: float32 [2, 1048576], P(None, 'amp'), may hold values from -6 to 6
- observable: float32 [1048576], P('amp'), may hold values from -6 to 6
- angles: float32 [2, 3], replicated, may hold values from -3.140625 to 3.140625
- gate_kinds: int32 [2, 32], replicated, may hold values from 0 to 2
Outputs:
- bra_state: float32 [2, 1048576], P(None, 'amp')
- grads: float32 [2, 3], replicated
Inputs may be any that keep to these rules, and one draw needn't show every extreme that they name: `gate_kinds`: 0 and 1 name rotations about Y with angles[l, 0] and angles[l, 1], 2 a rotation about Z with angles[l, 2]; entries for qubits at or above the number of qubits are not used.
All inputs are finite; a program needn't handle non-finite values.
Results may differ from a plain program's by a relative error of at most 0.0003.
Values sent between devices are 32-bit elements; how exact they have to be, the bound alone decides.
A program may use at most 128 MiB of HBM per device.

v0:
```python
import math

import jax
import jax.numpy as jnp
import numpy as np
from jax import lax
from jax.sharding import PartitionSpec as P


def from_partner(value, axis, apart):
    mask = 2**apart
    pairs = [(source, source ^ mask) for source in range(lax.axis_size(axis))]
    return lax.ppermute(value, axis, pairs)


def pair_tables():
    column = np.arange(128)
    flips = []
    signs = []
    for position in range(7):
        upper = column >> position & 1
        flip_table = np.zeros((128, 128), np.float32)
        flip_table[column, column ^ 1 << position] = np.where(upper == 0, -0.5, 0.5)
        flips.append(flip_table)
        signs.append((1 - 2 * upper).astype(np.float32))
    return (np.stack(flips), np.stack(signs))


def layout_map(local_bits, global_bits):
    local_map = list(range(local_bits))
    device_map = [local_bits + bit_num for bit_num in range(global_bits)]
    return (local_map, device_map)


def entangle_sign(local_bits, global_bits, device_id, amp_count):
    local_map, device_map = layout_map(local_bits, global_bits)
    amp_index = lax.iota(jnp.int32, amp_count)
    bit_values = [None] * (local_bits + global_bits)
    for position in range(local_bits):
        bit_values[local_map[position]] = amp_index >> position & 1
    for bit_num in range(global_bits):
        bit_values[device_map[bit_num]] = device_id >> bit_num & 1
    all_bits = local_bits + global_bits
    parity = jnp.zeros((amp_count,), jnp.int32)
    for qubit_id in range(all_bits):
        parity = parity + bit_values[qubit_id] * bit_values[(qubit_id + 1) % all_bits]
    return (1 - 2 * (parity & 1)).astype(jnp.float32)


def rotation_of(angles, gate_kinds, layer_id, qubit_id):
    kind_id = gate_kinds[layer_id, qubit_id]
    chosen = jnp.arange(angles.shape[1]) == kind_id
    rotation = jnp.sum(jnp.where(chosen, angles[layer_id], 0.0))
    return (kind_id, jnp.cos(0.5 * rotation), jnp.sin(0.5 * rotation))


def kind_vector(kind_id, kind_count):
    return (jnp.arange(kind_count) == kind_id).astype(jnp.float32)


def rotate_phase(values, cosine, sine_value):
    return jnp.stack(
        [cosine * values[0] - sine_value * values[1], cosine * values[1] + sine_value * values[0]]
    )


def rotate_position(ket_state, bra_state, position, qubit_id, layer_id, angles, gate_kinds):
    amp_count = ket_state.shape[1]
    fold_shape = (2, amp_count >> position + 1, 2, 1 << position)
    kind_id, cosine, sine_value = rotation_of(angles, gate_kinds, layer_id, qubit_id)

    def turn_y(operands):
        folded_ket, folded_bra = operands
        ket_low, ket_high = (folded_ket[:, :, 0], folded_ket[:, :, 1])
        bra_low, bra_high = (folded_bra[:, :, 0], folded_bra[:, :, 1])
        partial_value = 0.5 * jnp.sum(bra_high * ket_low - bra_low * ket_high)
        new_ket = jnp.stack(
            [cosine * ket_low + sine_value * ket_high, cosine * ket_high - sine_value * ket_low],
            axis=2,
        )
        new_bra = jnp.stack(
            [cosine * bra_low + sine_value * bra_high, cosine * bra_high - sine_value * bra_low],
            axis=2,
        )
        return (new_ket, new_bra, partial_value)

    def turn_z(operands):
        folded_ket, folded_bra = operands
        ket_low, ket_high = (folded_ket[:, :, 0], folded_ket[:, :, 1])
        bra_low, bra_high = (folded_bra[:, :, 0], folded_bra[:, :, 1])
        partial_value = 0.5 * (
            jnp.sum(bra_low[0] * ket_low[1] - bra_low[1] * ket_low[0])
            - jnp.sum(bra_high[0] * ket_high[1] - bra_high[1] * ket_high[0])
        )
        new_ket = jnp.stack(
            [
                rotate_phase(ket_low, cosine, sine_value),
                rotate_phase(ket_high, cosine, -sine_value),
            ],
            axis=2,
        )
        new_bra = jnp.stack(
            [
                rotate_phase(bra_low, cosine, sine_value),
                rotate_phase(bra_high, cosine, -sine_value),
            ],
            axis=2,
        )
        return (new_ket, new_bra, partial_value)

    new_ket, new_bra, partial_value = lax.cond(
        kind_id == 2, turn_z, turn_y, (ket_state.reshape(fold_shape), bra_state.reshape(fold_shape))
    )
    terms = partial_value * kind_vector(kind_id, angles.shape[1])
    return (new_ket.reshape(2, amp_count), new_bra.reshape(2, amp_count), terms)


def contract_rows(left, right):
    return lax.dot_general(
        left,
        right,
        (((0,), (0,)), ((), ())),
        precision=lax.Precision.HIGHEST,
        preferred_element_type=jnp.float32,
    )


def contract_cols(left, right):
    return lax.dot_general(
        left,
        right,
        (((1,), (1,)), ((), ())),
        precision=lax.Precision.HIGHEST,
        preferred_element_type=jnp.float32,
    )


def low_block(ket_state, bra_state, qubit_list, layer_id, angles, gate_kinds):
    amp_count = ket_state.shape[1]
    row_count = amp_count // 128
    flips, signs = pair_tables()
    ket_real = ket_state[0].reshape(row_count, 128)
    ket_imag = ket_state[1].reshape(row_count, 128)
    bra_real = bra_state[0].reshape(row_count, 128)
    bra_imag = bra_state[1].reshape(row_count, 128)
    gram_real = contract_rows(bra_real, ket_real) + contract_rows(bra_imag, ket_imag)
    gram_imag = contract_rows(bra_real, ket_imag) - contract_rows(bra_imag, ket_real)
    gram_diag = jnp.diagonal(gram_imag)
    terms = jnp.zeros((angles.shape[1],), jnp.float32)
    kron_real = None
    kron_imag = None
    for position in range(7):
        kind_id, cosine, sine_value = rotation_of(
            angles, gate_kinds, layer_id, qubit_list[position]
        )
        is_z = kind_id == 2
        partial_value = jnp.where(
            is_z, 0.5 * jnp.sum(signs[position] * gram_diag), jnp.sum(flips[position] * gram_real)
        )
        terms = terms + partial_value * kind_vector(kind_id, angles.shape[1])
        mat_y = jnp.stack([jnp.stack([cosine, sine_value]), jnp.stack([-sine_value, cosine])])
        zero_value = jnp.zeros_like(cosine)
        mat_zr = jnp.stack([jnp.stack([cosine, zero_value]), jnp.stack([zero_value, cosine])])
        mat_zi = jnp.stack(
            [jnp.stack([sine_value, zero_value]), jnp.stack([zero_value, -sine_value])]
        )
        mat_real = jnp.where(is_z, mat_zr, mat_y)
        mat_imag = jnp.where(is_z, mat_zi, jnp.zeros_like(mat_zi))
        if kron_real is None:
            kron_real, kron_imag = (mat_real, mat_imag)
        else:
            kron_real, kron_imag = (
                jnp.kron(mat_real, kron_real) - jnp.kron(mat_imag, kron_imag),
                jnp.kron(mat_real, kron_imag) + jnp.kron(mat_imag, kron_real),
            )

    def apply_block(real_rows, imag_rows):
        new_real = contract_cols(real_rows, kron_real) - contract_cols(imag_rows, kron_imag)
        new_imag = contract_cols(imag_rows, kron_real) + contract_cols(real_rows, kron_imag)
        return jnp.stack([new_real.reshape(amp_count), new_imag.reshape(amp_count)])

    return (apply_block(ket_real, ket_imag), apply_block(bra_real, bra_imag), terms)


def rotate_global(
    ket_state,
    bra_state,
    far_ket,
    far_bra,
    bit_num,
    qubit_id,
    device_id,
    layer_id,
    angles,
    gate_kinds,
):
    kind_id, cosine, sine_value = rotation_of(angles, gate_kinds, layer_id, qubit_id)
    orient = (1 - 2 * (device_id >> bit_num & 1)).astype(jnp.float32)

    def turn_y(operands):
        own_ket, own_bra, other_ket, other_bra = operands
        partial_value = 0.25 * orient * jnp.sum(other_bra * own_ket - own_bra * other_ket)
        return (
            cosine * own_ket + orient * sine_value * other_ket,
            cosine * own_bra + orient * sine_value * other_bra,
            partial_value,
        )

    def turn_z(operands):
        own_ket, own_bra, other_ket, other_bra = operands
        partial_value = 0.5 * orient * jnp.sum(own_bra[0] * own_ket[1] - own_bra[1] * own_ket[0])
        return (
            rotate_phase(own_ket, cosine, orient * sine_value),
            rotate_phase(own_bra, cosine, orient * sine_value),
            partial_value,
        )

    new_ket, new_bra, partial_value = lax.cond(
        kind_id == 2, turn_z, turn_y, (ket_state, bra_state, far_ket, far_bra)
    )
    return (new_ket, new_bra, partial_value * kind_vector(kind_id, angles.shape[1]))


def on_device(ket_state, observable, angles, gate_kinds):
    amp_count = ket_state.shape[1]
    local_bits = amp_count.bit_length() - 1
    group_size = lax.axis_size("amp")
    global_bits = group_size.bit_length() - 1
    device_id = lax.axis_index("amp")
    layer_count = angles.shape[0]
    kind_count = angles.shape[1]
    bra_state = 2.0 / math.sqrt(amp_count * group_size) * observable[None, :] * ket_state
    sign_cache = {}
    grads_local = jnp.zeros((layer_count, kind_count), jnp.float32)
    for sweep_id in range(layer_count):
        layer_id = layer_count - 1 - sweep_id
        layout = 0
        local_map, device_map = layout_map(local_bits, global_bits)
        if layout not in sign_cache:
            sign_cache[layout] = entangle_sign(local_bits, global_bits, device_id, amp_count)
        phase_sign = sign_cache[layout]
        ket_state = ket_state * phase_sign[None, :]
        bra_state = bra_state * phase_sign[None, :]
        ket_state, bra_state, layer_terms = low_block(
            ket_state, bra_state, local_map[:7], layer_id, angles, gate_kinds
        )
        for position in range(7, local_bits):
            ket_state, bra_state, partial_value = rotate_position(
                ket_state, bra_state, position, local_map[position], layer_id, angles, gate_kinds
            )
            layer_terms = layer_terms + partial_value
        for bit_num in range(global_bits):
            far_ket, far_bra = from_partner((ket_state, bra_state), "amp", bit_num)
            ket_state, bra_state, partial_value = rotate_global(
                ket_state,
                bra_state,
                far_ket,
                far_bra,
                bit_num,
                device_map[bit_num],
                device_id,
                layer_id,
                angles,
                gate_kinds,
            )
            layer_terms = layer_terms + partial_value
        grads_local = grads_local.at[layer_id].set(layer_terms)
    grads = lax.psum(grads_local, "amp")
    return (bra_state, grads)


def solution(mesh):
    placed = (P(None, "amp"), P("amp"), P(), P())
    return jax.shard_map(
        on_device, mesh=mesh, in_specs=placed, out_specs=(P(None, "amp"), P()), check_vma=False
    )
```

profile of v0, /device:TPU:0, one launch (start us, length us, event | category | flops | bytes accessed | tf_op | source)
XLA Modules:
  0.0 363.9 jit_solution(7483152363977186762)
XLA Ops:
  5.3 6.3 %fusion.150 = (f32[]{:T(128)}, f32[]{:T(128)}, f32[]{:T(128)}, f32[]{:T(128)}, f32[]{:T(128)}, /*index=5*/f32[]{:T(128)}, f32[]{:T(128)}, f32[]{:T(128)}, f32[]{:T(128)}) fusion(s32[]{:T(128)} %bitcast.199, f32[2,3]{1,0:T(2,128)S(1)} %copy-done.11, s32[]{:T(128)} %bitcast.206, s32[]{:T(128)} %bitcast.208, s32[]{:T(128)} %bitcast.209, s32[]{:T(128)} %bitcast.210, ...), kind=kLoop, calls=%fused_computation.857 | loop fusion | flops 72 | bytes 96 | tf_op jit(solution)/shard_map/reduce_sum | solution.py:53
  19.5 6.5 %fusion.149 = (f32[]{:T(128)}, f32[]{:T(128)}, f32[]{:T(128)}, f32[]{:T(128)}, f32[]{:T(128)}, /*index=5*/f32[]{:T(128)}, f32[]{:T(128)}, f32[]{:T(128)}, f32[]{:T(128)}) fusion(s32[]{:T(128)} %bitcast.200, f32[2,3]{1,0:T(2,128)S(1)} %copy-done.11, s32[]{:T(128)} %bitcast.245, s32[]{:T(128)} %bitcast.253, s32[]{:T(128)} %bitcast.261, s32[]{:T(128)} %bitcast.269, ...), kind=kLoop, calls=%fused_computation.856 | loop fusion | flops 72 | bytes 96 | tf_op jit(solution)/shard_map/reduce_sum | solution.py:53
  32.8 6.4 %fusion.148 = (f32[]{:T(128)}, f32[]{:T(128)}, f32[]{:T(128)}, f32[]{:T(128)}, f32[]{:T(128)}, /*index=5*/f32[]{:T(128)}, f32[]{:T(128)}, f32[]{:T(128)}, f32[]{:T(128)}) fusion(s32[]{:T(128)} %bitcast.201, f32[2,3]{1,0:T(2,128)S(1)} %copy-done.11, s32[]{:T(128)} %bitcast.215, s32[]{:T(128)} %bitcast.214, s32[]{:T(128)} %bitcast.213, s32[]{:T(128)} %bitcast.192, ...), kind=kLoop, calls=%fused_computation.855 | loop fusion | flops 72 | bytes 96 | tf_op jit(solution)/shard_map/reduce_sum | solution.py:53
  52.7 3.1 conditional.27
  58.5 4.8 %conditional.29 = (f32[]{:T(128)}, f32[2,8,2,2048]{3,2,1,0:T(2,128)S(1)}, f32[2,8,2,2048]{3,2,1,0:T(2,128)S(1)}) conditional(s32[]{:T(128)} %convert_element_type.167, (f32[2,16,2,1024]{3,2,1,0:T(2,128)S(1)}, f32[2,16,2,1024]{3,2,1,0:T(2,128)S(1)}, f32[]{:T(128)}) %tuple.335, (f32[2,16,2,1024]{3,2,1,0:T(2,128)S(1)}, ...), branch_computations={%region_26.28_spmd, %region_28.31_spmd} | conditional | flops 786433 | bytes 6684776 | solution.py:111
  63.3 3.1 conditional.30
  66.4 8.6 %conditional.31 = (f32[]{:T(128)}, f32[2,2,2,8192]{3,2,1,0:T(2,128)S(1)}, f32[2,2,2,8192]{3,2,1,0:T(2,128)S(1)}) conditional(s32[]{:T(128)} %convert_element_type.165, (f32[2,4,2,4096]{3,2,1,0:T(2,128)S(1)}, f32[2,4,2,4096]{3,2,1,0:T(2,128)S(1)}, f32[]{:T(128)}) %tuple.337, (f32[2,4,2,4096]{3,2,1,0:T(2,128)S(1)}, f32[2,4,2,4096]{3,2,1,0:T(2,128)S(1)}, ...), branch_computations={%region_38.40_spmd, %region_40.43_spmd} | conditional | flops 786433 | bytes 6684776 | solution.py:111
  75.0 5.0 %conditional.32 = (f32[]{:T(128)}, f32[2,1,2,16384]{3,2,1,0:T(2,128)S(1)}, f32[2,1,2,16384]{3,2,1,0:T(2,128)S(1)}) conditional(s32[]{:T(128)} %convert_element_type.164, (f32[2,2,2,8192]{3,2,1,0:T(2,128)S(1)}, f32[2,2,2,8192]{3,2,1,0:T(2,128)S(1)}, f32[]{:T(128)}) %tuple.338, (f32[2,2,2,8192]{3,2,1,0:T(2,128)S(1)}, ...), branch_computations={%region_44.46_spmd, %region_46.49_spmd} | conditional | flops 786433 | bytes 6684776 | solution.py:111
  80.0 6.4 %conditional.33 = (f32[]{:T(128)}, f32[2,32768]{1,0:T(2,128)S(1)}, f32[2,32768]{1,0:T(2,128)S(1)}) conditional(s32[]{:T(128)} %convert_element_type.163, (f32[2,1,2,16384]{3,2,1,0:T(2,128)S(1)}, f32[2,1,2,16384]{3,2,1,0:T(2,128)S(1)}, s32[]{:T(128)}, s32[3]{0:T(128)S(1)}, f32[3]{0:T(128)S(1)}, /*index=5*/f32[3]{0:T(128)S(1)}) %tuple.339, ...), branch_computations={%region_49.52_spmd, %region_52.56_spmd} | conditional | flops 786441 | bytes 4587668 | solution.py:111
  90.8 7.5 %fusion.146 = (f32[]{:T(128)}, f32[]{:T(128)}, f32[]{:T(128)}, f32[]{:T(128)}, f32[]{:T(128)}, /*index=5*/f32[]{:T(128)}, f32[]{:T(128)}, f32[]{:T(128)}, f32[]{:T(128)}, f32[]{:T(128)}, /*index=10*/f32[]{:T(128)}) fusion(s32[]{:T(128)} %bitcast.203, f32[2,3]{1,0:T(2,128)S(1)} %copy-done.11, s32[]{:T(128)} %bitcast.204, s32[]{:T(128)} %bitcast.205, ...), kind=kLoop, calls=%fused_computation.853 | loop fusion | flops 88 | bytes 100 | tf_op jit(solution)/shard_map/reduce_sum | solution.py:53
  113.1 5.5 %collective-permute-done.2 = f32[2,32768]{1,0:T(2,128)S(1)} collective-permute-done((f32[2,32768]{1,0:T(2,128)S(1)}, f32[2,32768]{1,0:T(2,128)S(1)}, u32[]{:S(2)}, u32[]{:S(2)}) %collective-permute-start.2) | collective-permute-done | bytes 262176 | tf_op jit(solution)/shard_map/ppermute | solution.py:13
  118.5 5.0 %collective-permute-done.3 = f32[2,32768]{1,0:T(2,128)S(1)} collective-permute-done((f32[2,32768]{1,0:T(2,128)S(1)}, f32[2,32768]{1,0:T(2,128)S(1)}, u32[]{:S(2)}, u32[]{:S(2)}) %collective-permute-start.3) | collective-permute-done | bytes 262176 | tf_op jit(solution)/shard_map/ppermute | solution.py:13
  129.3 5.4 %collective-permute-done.4 = f32[2,32768]{1,0:T(2,128)S(1)} collective-permute-done((f32[2,32768]{1,0:T(2,128)S(1)}, f32[2,32768]{1,0:T(2,128)S(1)}, u32[]{:S(2)}, u32[]{:S(2)}) %collective-permute-start.4) | collective-permute-done | bytes 262176 | tf_op jit(solution)/shard_map/ppermute | solution.py:13
  134.8 4.2 %collective-permute-done.5 = f32[2,32768]{1,0:T(2,128)S(1)} collective-permute-done((f32[2,32768]{1,0:T(2,128)S(1)}, f32[2,32768]{1,0:T(2,128)S(1)}, u32[]{:S(2)}, u32[]{:S(2)}) %collective-permute-start.5) | collective-permute-done | bytes 262176 | tf_op jit(solution)/shard_map/ppermute | solution.py:13
  144.4 4.8 %collective-permute-done.6 = f32[2,32768]{1,0:T(2,128)S(1)} collective-permute-done((f32[2,32768]{1,0:T(2,128)S(1)}, f32[2,32768]{1,0:T(2,128)S(1)}, u32[]{:S(2)}, u32[]{:S(2)}) %collective-permute-start.6) | collective-permute-done | bytes 262176 | tf_op jit(solution)/shard_map/ppermute | solution.py:13
  149.1 3.3 collective-permute-done.7
  168.9 4.1 %collective-permute-done.8 = f32[2,32768]{1,0:T(2,128)S(1)} collective-permute-done((f32[2,32768]{1,0:T(2,128)S(1)}, f32[2,32768]{1,0:T(2,128)S(1)}, u32[]{:S(2)}, u32[]{:S(2)}) %collective-permute-start.8) | collective-permute-done | bytes 262176 | tf_op jit(solution)/shard_map/ppermute | solution.py:13
  173.0 5.1 %collective-permute-done.9 = f32[2,32768]{1,0:T(2,128)S(1)} collective-permute-done((f32[2,32768]{1,0:T(2,128)S(1)}, f32[2,32768]{1,0:T(2,128)S(1)}, u32[]{:S(2)}, u32[]{:S(2)}) %collective-permute-start.9) | collective-permute-done | bytes 262176 | tf_op jit(solution)/shard_map/ppermute | solution.py:13
  183.0 3.5 conditional.39
  186.6 5.1 %conditional.40 = (f32[]{:T(128)}, f32[2,32,2,512]{3,2,1,0:T(2,128)S(1)}, f32[2,32,2,512]{3,2,1,0:T(2,128)S(1)}) conditional(s32[]{:T(128)} %convert_element_type.156, (f32[2,64,2,256]{3,2,1,0:T(2,128)S(1)}, f32[2,64,2,256]{3,2,1,0:T(2,128)S(1)}, f32[]{:T(128)}) %tuple.351, (f32[2,64,2,256]{3,2,1,0:T(2,128)S(1)}, ...), branch_computations={%region_95.97_spmd, %region_97.100_spmd} | conditional | flops 786433 | bytes 6684776 | solution.py:111
  191.7 5.2 %conditional.41 = (f32[]{:T(128)}, f32[2,16,2,1024]{3,2,1,0:T(2,128)S(1)}, f32[2,16,2,1024]{3,2,1,0:T(2,128)S(1)}) conditional(s32[]{:T(128)} %convert_element_type.155, (f32[2,32,2,512]{3,2,1,0:T(2,128)S(1)}, f32[2,32,2,512]{3,2,1,0:T(2,128)S(1)}, f32[]{:T(128)}) %tuple.352, (f32[2,32,2,512]{3,2,1,0:T(2,128)S(1)}, ...), branch_computations={%region_101.103_spmd, %region_103.106_spmd} | conditional | flops 786433 | bytes 6684776 | solution.py:111
  196.9 5.7 %conditional.42 = (f32[]{:T(128)}, f32[2,8,2,2048]{3,2,1,0:T(2,128)S(1)}, f32[2,8,2,2048]{3,2,1,0:T(2,128)S(1)}) conditional(s32[]{:T(128)} %convert_element_type.154, (f32[2,16,2,1024]{3,2,1,0:T(2,128)S(1)}, f32[2,16,2,1024]{3,2,1,0:T(2,128)S(1)}, f32[]{:T(128)}) %tuple.353, (f32[2,16,2,1024]{3,2,1,0:T(2,128)S(1)}, ...), branch_computations={%region_107.109_spmd, %region_109.112_spmd} | conditional | flops 786433 | bytes 6684776 | solution.py:111
  202.5 5.1 %conditional.43 = (f32[]{:T(128)}, f32[2,4,2,4096]{3,2,1,0:T(2,128)S(1)}, f32[2,4,2,4096]{3,2,1,0:T(2,128)S(1)}) conditional(s32[]{:T(128)} %convert_element_type.76, (f32[2,8,2,2048]{3,2,1,0:T(2,128)S(1)}, f32[2,8,2,2048]{3,2,1,0:T(2,128)S(1)}, f32[]{:T(128)}) %tuple.354, (f32[2,8,2,2048]{3,2,1,0:T(2,128)S(1)}, ...), branch_computations={%region_113.115_spmd, %region_115.118_spmd} | conditional | flops 786433 | bytes 6684776 | solution.py:111
  207.6 3.3 conditional.44
  210.9 3.3 conditional.45
  214.3 10.9 %conditional.46 = (f32[]{:T(128)}, f32[2,32768]{1,0:T(2,128)S(1)}, f32[2,32768]{1,0:T(2,128)S(1)}) conditional(s32[]{:T(128)} %convert_element_type.73, (f32[2,1,2,16384]{3,2,1,0:T(2,128)S(1)}, f32[2,1,2,16384]{3,2,1,0:T(2,128)S(1)}, s32[]{:T(128)}, s32[3]{0:T(128)S(1)}, f32[3]{0:T(128)S(1)}, /*index=5*/f32[3]{0:T(128)S(1)}) %tuple.357, ...), branch_computations={%region_130.133_spmd, %region_133.137_spmd} | conditional | flops 786441 | bytes 4587668 | solution.py:111
  248.3 5.1 %collective-permute-done.14 = f32[2,32768]{1,0:T(2,128)S(1)} collective-permute-done((f32[2,32768]{1,0:T(2,128)S(1)}, f32[2,32768]{1,0:T(2,128)S(1)}, u32[]{:S(2)}, u32[]{:S(2)}) %collective-permute-start.14) | collective-permute-done | bytes 262176 | tf_op jit(solution)/shard_map/ppermute | solution.py:13
  253.4 3.9 %collective-permute-done.15 = f32[2,32768]{1,0:T(2,128)S(1)} collective-permute-done((f32[2,32768]{1,0:T(2,128)S(1)}, f32[2,32768]{1,0:T(2,128)S(1)}, u32[]{:S(2)}, u32[]{:S(2)}) %collective-permute-start.15) | collective-permute-done | bytes 262176 | tf_op jit(solution)/shard_map/ppermute | solution.py:13
  263.0 5.4 %collective-permute-done.16 = f32[2,32768]{1,0:T(2,128)S(1)} collective-permute-done((f32[2,32768]{1,0:T(2,128)S(1)}, f32[2,32768]{1,0:T(2,128)S(1)}, u32[]{:S(2)}, u32[]{:S(2)}) %collective-permute-start.16) | collective-permute-done | bytes 262176 | tf_op jit(solution)/shard_map/ppermute | solution.py:13
  294.7 12.7 %fusion.188 = f32[1,3]{1,0:T(1,128)S(1)} fusion(f32[]{:T(128)S(6)} %mul.7475, s32[]{:T(128)} %bitcast.206, f32[]{:T(128)S(6)} %mul.7471, s32[]{:T(128)} %bitcast.208, f32[]{:T(128)S(6)} %mul.7467, s32[]{:T(128)} %bitcast.209, f32[]{:T(128)S(6)} %mul.7463, s32[]{:T(128)} %bitcast.210, f32[]{:T(128)S(6)} %mul.7459, s32[]{:T(128)} %bitcast.211, f32[]{:T(128)S(6)} %mul.7455, ...), kind=kLoop, calls=%fused_computation.895 | loop fusion | flops 177 | bytes 172 | tf_op jit(solution)/shard_map/add | solution.py:266
  311.4 12.4 %fusion.169 = f32[1,3]{1,0:T(1,128)S(1)} fusion(f32[]{:T(128)S(6)} %mul.7403, s32[]{:T(128)} %bitcast.192, f32[]{:T(128)S(6)} %mul.7399, s32[]{:T(128)} %bitcast.194, f32[]{:T(128)S(6)} %mul.7395, s32[]{:T(128)} %bitcast.195, f32[]{:T(128)S(6)} %mul.7391, s32[]{:T(128)} %bitcast.196, f32[]{:T(128)S(6)} %mul.7387, s32[]{:T(128)} %bitcast.197, f32[]{:T(128)S(6)} %mul.7383, ...), kind=kLoop, calls=%fused_computation.876 | loop fusion | flops 177 | bytes 172 | tf_op jit(solution)/shard_map/add | solution.py:266
  323.9 39.6 %psum.7 = f32[2,3]{1,0:T(2,128)} all-reduce(f32[2,3]{1,0:T(2,128)S(1)} %pad_maximum_fusion.79), channel_id=1, replica_groups=mesh['amp'=32] {'amp'}, use_global_device_ids=true, to_apply=%region_190.191 | all-reduce | flops 6 | bytes 48 | tf_op jit(solution)/shard_map/psum | solution.py:268
  (412 shorter events, 129.5 us)
Async XLA Ops:
  86.4 21.0 %collective-permute-start.1 = (f32[2,32768]{1,0:T(2,128)S(1)}, f32[2,32768]{1,0:T(2,128)S(1)}, u32[]{:S(2)}, u32[]{:S(2)}) collective-permute-start(f32[2,32768]{1,0:T(2,128)S(1)} %get-tuple-element.1402), channel_id=1, source_target_pairs={{0,1},{1,0},{2,3},{3,2},{4,5},{5,4},{6,7},{7,6},{8,9},{9,8},{10,11... | collective-permute-start | bytes 786440 | tf_op jit(solution)/shard_map/ppermute | solution.py:13
  87.0 20.4 %collective-permute-start = (f32[2,32768]{1,0:T(2,128)S(1)}, f32[2,32768]{1,0:T(2,128)S(1)}, u32[]{:S(2)}, u32[]{:S(2)}) collective-permute-start(f32[2,32768]{1,0:T(2,128)S(1)} %get-tuple-element.1401), channel_id=1, source_target_pairs={{0,1},{1,0},{2,3},{3,2},{4,5},{5,4},{6,7},{7,6},{8,9},{9,8},{10,11... | collective-permute-start | bytes 786440 | tf_op jit(solution)/shard_map/ppermute | solution.py:13
  108.5 10.0 %collective-permute-start.2 = (f32[2,32768]{1,0:T(2,128)S(1)}, f32[2,32768]{1,0:T(2,128)S(1)}, u32[]{:S(2)}, u32[]{:S(2)}) collective-permute-start(f32[2,32768]{1,0:T(2,128)S(1)} %get-tuple-element.1038), channel_id=1, source_target_pairs={{0,2},{1,3},{2,0},{3,1},{4,6},{5,7},{6,4},{7,5},{8,10},{9,11},{10,... | collective-permute-start | bytes 786440 | tf_op jit(solution)/shard_map/ppermute | solution.py:13
  111.4 12.2 %collective-permute-start.3 = (f32[2,32768]{1,0:T(2,128)S(1)}, f32[2,32768]{1,0:T(2,128)S(1)}, u32[]{:S(2)}, u32[]{:S(2)}) collective-permute-start(f32[2,32768]{1,0:T(2,128)S(1)} %get-tuple-element.1039), channel_id=1, source_target_pairs={{0,2},{1,3},{2,0},{3,1},{4,6},{5,7},{6,4},{7,5},{8,10},{9,11},{10,... | collective-permute-start | bytes 786440 | tf_op jit(solution)/shard_map/ppermute | solution.py:13
  125.5 9.2 %collective-permute-start.4 = (f32[2,32768]{1,0:T(2,128)S(1)}, f32[2,32768]{1,0:T(2,128)S(1)}, u32[]{:S(2)}, u32[]{:S(2)}) collective-permute-start(f32[2,32768]{1,0:T(2,128)S(1)} %get-tuple-element.1040), channel_id=1, source_target_pairs={{0,4},{1,5},{2,6},{3,7},{4,0},{5,1},{6,2},{7,3},{8,12},{9,13},{10,... | collective-permute-start | bytes 786440 | tf_op jit(solution)/shard_map/ppermute | solution.py:13
  127.4 11.6 %collective-permute-start.5 = (f32[2,32768]{1,0:T(2,128)S(1)}, f32[2,32768]{1,0:T(2,128)S(1)}, u32[]{:S(2)}, u32[]{:S(2)}) collective-permute-start(f32[2,32768]{1,0:T(2,128)S(1)} %get-tuple-element.1041), channel_id=1, source_target_pairs={{0,4},{1,5},{2,6},{3,7},{4,0},{5,1},{6,2},{7,3},{8,12},{9,13},{10,... | collective-permute-start | bytes 786440 | tf_op jit(solution)/shard_map/ppermute | solution.py:13
  140.0 9.2 %collective-permute-start.6 = (f32[2,32768]{1,0:T(2,128)S(1)}, f32[2,32768]{1,0:T(2,128)S(1)}, u32[]{:S(2)}, u32[]{:S(2)}) collective-permute-start(f32[2,32768]{1,0:T(2,128)S(1)} %get-tuple-element.1042), channel_id=1, source_target_pairs={{0,8},{1,9},{2,10},{3,11},{4,12},{5,13},{6,14},{7,15},{8,0},{9,1},... | collective-permute-start | bytes 786440 | tf_op jit(solution)/shard_map/ppermute | solution.py:13
  141.5 10.9 %collective-permute-start.7 = (f32[2,32768]{1,0:T(2,128)S(1)}, f32[2,32768]{1,0:T(2,128)S(1)}, u32[]{:S(2)}, u32[]{:S(2)}) collective-permute-start(f32[2,32768]{1,0:T(2,128)S(1)} %get-tuple-element.1043), channel_id=1, source_target_pairs={{0,8},{1,9},{2,10},{3,11},{4,12},{5,13},{6,14},{7,15},{8,0},{9,1},... | collective-permute-start | bytes 786440 | tf_op jit(solution)/shard_map/ppermute | solution.py:13
  154.3 18.7 %collective-permute-start.8 = (f32[2,32768]{1,0:T(2,128)S(1)}, f32[2,32768]{1,0:T(2,128)S(1)}, u32[]{:S(2)}, u32[]{:S(2)}) collective-permute-start(f32[2,32768]{1,0:T(2,128)S(1)} %get-tuple-element.1044), channel_id=1, source_target_pairs={{0,16},{1,17},{2,18},{3,19},{4,20},{5,21},{6,22},{7,23},{8,24},{9,... | collective-permute-start | bytes 786440 | tf_op jit(solution)/shard_map/ppermute | solution.py:13
  156.7 21.5 %collective-permute-start.9 = (f32[2,32768]{1,0:T(2,128)S(1)}, f32[2,32768]{1,0:T(2,128)S(1)}, u32[]{:S(2)}, u32[]{:S(2)}) collective-permute-start(f32[2,32768]{1,0:T(2,128)S(1)} %get-tuple-element.1045), channel_id=1, source_target_pairs={{0,16},{1,17},{2,18},{3,19},{4,20},{5,21},{6,22},{7,23},{8,24},{9,... | collective-permute-start | bytes 786440 | tf_op jit(solution)/shard_map/ppermute | solution.py:13
  225.2 2.8 collective-permute-start.11
  225.3 2.7 collective-permute-start.10
  229.0 12.4 %collective-permute-start.12 = (f32[2,32768]{1,0:T(2,128)S(1)}, f32[2,32768]{1,0:T(2,128)S(1)}, u32[]{:S(2)}, u32[]{:S(2)}) collective-permute-start(f32[2,32768]{1,0:T(2,128)S(1)} %get-tuple-element.1064), channel_id=1, source_target_pairs={{0,2},{1,3},{2,0},{3,1},{4,6},{5,7},{6,4},{7,5},{8,10},{9,11},{10,... | collective-permute-start | bytes 786440 | tf_op jit(solution)/shard_map/ppermute | solution.py:13
  229.9 13.0 %collective-permute-start.13 = (f32[2,32768]{1,0:T(2,128)S(1)}, f32[2,32768]{1,0:T(2,128)S(1)}, u32[]{:S(2)}, u32[]{:S(2)}) collective-permute-start(f32[2,32768]{1,0:T(2,128)S(1)} %get-tuple-element.1065), channel_id=1, source_target_pairs={{0,2},{1,3},{2,0},{3,1},{4,6},{5,7},{6,4},{7,5},{8,10},{9,11},{10,... | collective-permute-start | bytes 786440 | tf_op jit(solution)/shard_map/ppermute | solution.py:13
  244.2 9.2 %collective-permute-start.14 = (f32[2,32768]{1,0:T(2,128)S(1)}, f32[2,32768]{1,0:T(2,128)S(1)}, u32[]{:S(2)}, u32[]{:S(2)}) collective-permute-start(f32[2,32768]{1,0:T(2,128)S(1)} %get-tuple-element.1066), channel_id=1, source_target_pairs={{0,4},{1,5},{2,6},{3,7},{4,0},{5,1},{6,2},{7,3},{8,12},{9,13},{10,... | collective-permute-start | bytes 786440 | tf_op jit(solution)/shard_map/ppermute | solution.py:13
  245.2 12.1 %collective-permute-start.15 = (f32[2,32768]{1,0:T(2,128)S(1)}, f32[2,32768]{1,0:T(2,128)S(1)}, u32[]{:S(2)}, u32[]{:S(2)}) collective-permute-start(f32[2,32768]{1,0:T(2,128)S(1)} %get-tuple-element.1067), channel_id=1, source_target_pairs={{0,4},{1,5},{2,6},{3,7},{4,0},{5,1},{6,2},{7,3},{8,12},{9,13},{10,... | collective-permute-start | bytes 786440 | tf_op jit(solution)/shard_map/ppermute | solution.py:13
  259.1 2.2 copy-start.15
  259.1 2.2 copy-start.16
  259.1 2.2 copy-start.17
  259.1 2.2 copy-start.18
  259.2 9.2 %collective-permute-start.16 = (f32[2,32768]{1,0:T(2,128)S(1)}, f32[2,32768]{1,0:T(2,128)S(1)}, u32[]{:S(2)}, u32[]{:S(2)}) collective-permute-start(f32[2,32768]{1,0:T(2,128)S(1)} %get-tuple-element.1068), channel_id=1, source_target_pairs={{0,8},{1,9},{2,10},{3,11},{4,12},{5,13},{6,14},{7,15},{8,0},{9,1},... | collective-permute-start | bytes 786440 | tf_op jit(solution)/shard_map/ppermute | solution.py:13
  259.3 12.1 %collective-permute-start.17 = (f32[2,32768]{1,0:T(2,128)S(1)}, f32[2,32768]{1,0:T(2,128)S(1)}, u32[]{:S(2)}, u32[]{:S(2)}) collective-permute-start(f32[2,32768]{1,0:T(2,128)S(1)} %get-tuple-element.1069), channel_id=1, source_target_pairs={{0,8},{1,9},{2,10},{3,11},{4,12},{5,13},{6,14},{7,15},{8,0},{9,1},... | collective-permute-start | bytes 786440 | tf_op jit(solution)/shard_map/ppermute | solution.py:13
  271.4 13.3 %copy-start.5 = (f32[128,128]{1,0:T(8,128)S(1)}, f32[128,128]{1,0:T(8,128)}, u32[]{:S(2)}) copy-start(f32[128,128]{1,0:T(8,128)} %constant.402.clone) | copy-start | bytes 196612
  271.4 13.3 %copy-start.6 = (f32[128,128]{1,0:T(8,128)S(1)}, f32[128,128]{1,0:T(8,128)}, u32[]{:S(2)}) copy-start(f32[128,128]{1,0:T(8,128)} %constant.400.clone) | copy-start | bytes 196612
  271.4 13.3 %copy-start.7 = (f32[128,128]{1,0:T(8,128)S(1)}, f32[128,128]{1,0:T(8,128)}, u32[]{:S(2)}) copy-start(f32[128,128]{1,0:T(8,128)} %constant.398.clone) | copy-start | bytes 196612
  271.4 13.3 %copy-start.8 = (f32[128,128]{1,0:T(8,128)S(1)}, f32[128,128]{1,0:T(8,128)}, u32[]{:S(2)}) copy-start(f32[128,128]{1,0:T(8,128)} %constant.396.clone) | copy-start | bytes 196612
  271.4 13.3 %copy-start.9 = (f32[128,128]{1,0:T(8,128)S(1)}, f32[128,128]{1,0:T(8,128)}, u32[]{:S(2)}) copy-start(f32[128,128]{1,0:T(8,128)} %constant.394.clone) | copy-start | bytes 196612
  271.4 13.3 %copy-start.10 = (f32[128,128]{1,0:T(8,128)S(1)}, f32[128,128]{1,0:T(8,128)}, u32[]{:S(2)}) copy-start(f32[128,128]{1,0:T(8,128)} %constant.392.clone) | copy-start | bytes 196612
  272.5 12.3 %copy-start.4 = (f32[128,128]{1,0:T(8,128)S(1)}, f32[128,128]{1,0:T(8,128)}, u32[]{:S(2)}) copy-start(f32[128,128]{1,0:T(8,128)} %constant.404.clone) | copy-start | bytes 196612
  272.5 37.3 %collective-permute-start.18 = (f32[2,32768]{1,0:T(2,128)S(1)}, f32[2,32768]{1,0:T(2,128)S(1)}, u32[]{:S(2)}, u32[]{:S(2)}) collective-permute-start(f32[2,32768]{1,0:T(2,128)S(1)} %get-tuple-element.1070), channel_id=1, source_target_pairs={{0,16},{1,17},{2,18},{3,19},{4,20},{5,21},{6,22},{7,23},{8,24},{9,... | collective-permute-start | bytes 786440 | tf_op jit(solution)/shard_map/ppermute | solution.py:13
  274.2 35.6 %collective-permute-start.19 = (f32[2,32768]{1,0:T(2,128)S(1)}, f32[2,32768]{1,0:T(2,128)S(1)}, u32[]{:S(2)}, u32[]{:S(2)}) collective-permute-start(f32[2,32768]{1,0:T(2,128)S(1)} %get-tuple-element.1071), channel_id=1, source_target_pairs={{0,16},{1,17},{2,18},{3,19},{4,20},{5,21},{6,22},{7,23},{8,24},{9,... | collective-permute-start | bytes 786440 | tf_op jit(solution)/shard_map/ppermute | solution.py:13
  310.8 52.7 %copy-start.2 = (f32[2,32768]{1,0:T(2,128)}, f32[2,32768]{1,0:T(2,128)S(1)}, u32[]{:S(2)}) copy-start(f32[2,32768]{1,0:T(2,128)S(1)} %get-tuple-element.1020) | copy-start | bytes 786436
  (7 other events, 9.7 us)
where the time goes:
time: 366 us; the launch traced here: 364 us
  other arithmetic  100 us (27%)
  between operations  79.5 us (22%)
  waiting for transfers between devices  56.3 us (15%)
  blocking collectives  39.6 us (11%)
  loops' own time  30.8 us (8%)
  local copies, waits for them, and re-layouts  29 us (8%)
  starting transfers between devices  20.4 us (6%)
  matrix products  8.27 us (2%)
    ppermute x20, waiting for transfers between devices, from_partner(): return lax.ppermute(value, axis, pairs)  56.3 us
    psum x1, blocking collectives, on_device(): grads = lax.psum(grads_local, 'amp')  39.6 us
    another operation x16, loops' own time, rotate_position(): lax.cond(kind_id == 2, turn_z, turn_y, (ket_state.reshape(fold_shape), br...  30.3 us
    reduce_sum x6, other arithmetic, rotation_of(): rotation = jnp.sum(jnp.where(chosen, angles[layer_id], 0.0))  29.1 us
    add x2, other arithmetic, on_device(): layer_terms = layer_terms + partial_value  25.1 us
    ppermute x20, starting transfers between devices, from_partner(): return lax.ppermute(value, axis, pairs)  20.4 us
    add x9, other arithmetic, turn_y(): cosine * bra_low + sine_value * bra_high  8.21 us
  transfers between devices with their start and end apart: 20, of which 13 were waited for; matrix products, arithmetic and copies ran while one was open for 8% of the time, Pallas kernels for 0%

commit v1 on v0

--- a/solution.py
+++ b/solution.py
@@ -1,10 +1,17 @@
+import functools
 import math
 
 import jax
 import jax.numpy as jnp
 import numpy as np
 from jax import lax
+from jax.experimental import pallas as pl
+from jax.experimental.pallas import tpu as pltpu
 from jax.sharding import PartitionSpec as P
+
+MESH = pl.DeviceIdType.MESH
+LANE, SUB, MAJOR, DEVICE = range(4)
+LANE_BITS, SUB_BITS = 7, 3
 
 
 def from_partner(value, axis, apart):
@@ -269,8 +276,326 @@
     return (bra_state, grads)
 
 
+def layouts(major_bits, global_bits):
+    low = LANE_BITS + SUB_BITS
+    local_bits = low + major_bits
+    home, away = {}, {}
+    for q in range(LANE_BITS):
+        home[q] = away[q] = (LANE, q)
+    home[LANE_BITS] = away[LANE_BITS] = (SUB, 0)
+    for bit, q in ((1, local_bits - 2), (2, local_bits - 1)):
+        home[q] = away[q] = (SUB, bit)
+    moved = list(range(low, local_bits - 2)) + [low - 2, low - 1]
+    for bit, q in enumerate(moved):
+        home[q], away[q] = (MAJOR, bit), (DEVICE, bit)
+    for bit in range(global_bits):
+        home[local_bits + bit], away[local_bits + bit] = (DEVICE, bit), (MAJOR, bit)
+    return home, away
+
+
+def split_major(x, bit):
+    fold = x.reshape((x.shape[0] >> bit + 1, 2, 1 << bit) + x.shape[1:])
+    return fold[:, 0], fold[:, 1]
+
+
+def join_major(x0, x1):
+    out = jnp.stack([x0, x1], axis=1)
+    return out.reshape((-1,) + out.shape[3:])
+
+
+def minor_bit(axis, bit):
+    return lax.broadcasted_iota(jnp.int32, (1, 8, 128), 1 if axis == SUB else 2) >> bit & 1
+
+
+def minor_sign(axis, bit):
+    return (1 - 2 * minor_bit(axis, bit)).astype(jnp.float32)
+
+
+def shifted(x, axis, by):
+    dim = 1 if axis == SUB else 2
+    return pltpu.roll(x, by % x.shape[dim], dim)
+
+
+def partner(x, axis, bit):
+    step = 1 << bit
+    up = shifted(x, axis, -step)
+    if 2 * step == x.shape[1 if axis == SUB else 2]:
+        return up
+    return jnp.where(minor_bit(axis, bit) == 0, up, shifted(x, axis, step))
+
+
+def swap_bits(x, major, sub):
+    x0, x1 = split_major(x, major)
+    lower = minor_bit(SUB, sub) == 0
+
+    def roll3(y, by):
+        z = y.reshape((-1,) + y.shape[2:])
+        return shifted(z, SUB, by).reshape(y.shape)
+
+    step = 1 << sub
+    return join_major(jnp.where(lower, x0, roll3(x1, step)), jnp.where(lower, roll3(x0, -step), x1))
+
+
+def gate(state, place, coef):
+    re, im = state
+    axis, bit = place
+    c, sy, sz = coef
+    if axis == MAJOR:
+        r0, r1 = split_major(re, bit)
+        i0, i1 = split_major(im, bit)
+        return (
+            join_major(c * r0 + sy * r1 - sz * i0, c * r1 - sy * r0 + sz * i1),
+            join_major(c * i0 + sy * i1 + sz * r0, c * i1 - sy * i0 - sz * r1),
+        )
+    z = minor_sign(axis, bit)
+    zy, zz = sy * z, sz * z
+    return (
+        c * re + zy * partner(re, axis, bit) - zz * im,
+        c * im + zy * partner(im, axis, bit) + zz * re,
+    )
+
+
+def terms(bra, ket, place, w, w_sum):
+    axis, bit = place
+    if axis == MAJOR:
+        y = 0.0
+        for b, k in zip(bra, ket):
+            b0, b1 = split_major(b, bit)
+            k0, k1 = split_major(k, bit)
+            y = y + jnp.sum(b1 * k0 - b0 * k1, axis=(0, 1))
+        w0, w1 = split_major(w, bit)
+        return 0.5 * y, 0.5 * jnp.sum(w0 - w1, axis=(0, 1))
+    z = 0.5 * minor_sign(axis, bit)[0]
+    y = sum(jnp.sum(b * partner(k, axis, bit), axis=0) for b, k in zip(bra, ket))
+    return -z * y, z * w_sum
+
+
+def edge_sign(place, qubits, edges, majors, me):
+    shape = (majors, 8, 128)
+    parts = {
+        LANE: lax.broadcasted_iota(jnp.int32, shape, 2),
+        SUB: lax.broadcasted_iota(jnp.int32, shape, 1),
+        MAJOR: lax.broadcasted_iota(jnp.int32, shape, 0),
+        DEVICE: me,
+    }
+    bits = [parts[place[q][0]] >> place[q][1] & 1 for q in range(qubits)]
+    parity = jnp.zeros(shape, jnp.int32)
+    for q in edges:
+        parity = parity + bits[q] * bits[(q + 1) % qubits]
+    return (1 - 2 * (parity & 1)).astype(jnp.float32)
+
+
+def half_turn(angle):
+    x = 0.5 * angle
+    x2 = x * x
+    cosine, sine = 0.0, 0.0
+    for n in range(8, -1, -1):
+        cosine = cosine * x2 + (-1.0) ** n / math.factorial(2 * n)
+        sine = sine * x2 + (-1.0) ** n / math.factorial(2 * n + 1)
+    return cosine, sine * x
+
+
+def kernel(
+    n, qubits, angles, kinds, ket_ref, obs_ref, out_ref, grads_ref,
+    sent1, held1, sent2, held2, gsent, gheld,
+    send1, recv1, send2, recv2, gsend, grecv,
+):
+    me = lax.axis_index("amp")
+    majors = n
+    major_bits = n.bit_length() - 1
+    local_bits = LANE_BITS + SUB_BITS + major_bits
+    home, away = layouts(major_bits, qubits - local_bits)
+    scale = 2.0 / math.sqrt(2**qubits)
+
+    barrier = pltpu.get_barrier_semaphore()
+
+    @pl.loop(1, n)
+    def _(k):
+        pl.semaphore_signal(barrier, inc=1, device_id=((me + k) % n,), device_id_type=MESH)
+
+    rows = 8 * majors
+    raw = [
+        ket_ref[pl.ds(0, rows, stride=2), :],
+        ket_ref[pl.ds(1, rows, stride=2), :],
+        obs_ref[...],
+    ]
+    for part, value in enumerate(raw):
+        value = value.reshape(majors, 8, 128)
+        for bit in (1, 2):
+            value = swap_bits(value, major_bits - 3 + bit, bit)
+        sent1[:, part] = value
+
+    pl.semaphore_wait(barrier, n - 1)
+
+    def exchange(source, target, send, recv, whole):
+        def copy(k, block, slot):
+            return pltpu.make_async_remote_copy(
+                src_ref=source if whole else source.at[block],
+                dst_ref=target.at[slot],
+                send_sem=send.at[k],
+                recv_sem=recv.at[k],
+                device_id=((me + k) % n,),
+                device_id_type=MESH,
+            )
+
+        def start():
+            @pl.loop(1, n)
+            def _(k):
+                copy(k, (me + k) % n, me).start()
+
+        def arrive():
+            @pl.loop(1, n)
+            def _(k):
+                copy(k, (me + k) % n, (me + n - k) % n).wait_recv()
+
+        def depart():
+            @pl.loop(1, n)
+            def _(k):
+                copy(k, (me + k) % n, me).wait_send()
+
+        return start, arrive, depart
+
+    start1, arrive1, depart1 = exchange(sent1, held1, send1, recv1, False)
+    start2, arrive2, depart2 = exchange(sent2, held2, send2, recv2, False)
+    gstart, garrive, gdepart = exchange(gsent, gheld, gsend, grecv, True)
+    start1()
+    held1[me] = sent1[me]
+
+    layers, kind_count = angles.shape
+    turns = [[half_turn(angles[l, k]) for k in range(kind_count)] for l in range(layers)]
+    coefs, shares = [], []
+    for l in range(layers):
+        row, share = [], []
+        for q in range(qubits):
+            kind = kinds[l, q]
+            is_kind = [jnp.where(kind == k, 1.0, 0.0) for k in range(kind_count)]
+            c = sum(is_kind[k] * turns[l][k][0] for k in range(kind_count))
+            sy = sum(is_kind[k] * turns[l][k][1] for k in range(kind_count - 1))
+            row.append((c, sy, is_kind[-1] * turns[l][-1][1]))
+            share.append(is_kind)
+        coefs.append(row)
+        shares.append(share)
+
+    sums = [[jnp.zeros((8, 128), jnp.float32) for _ in range(kind_count)] for _ in range(layers)]
+
+    def add_terms(l, chosen, place, bra, ket):
+        w = bra[0] * ket[1] - bra[1] * ket[0]
+        w_sum = jnp.sum(w, axis=0)
+        for q in chosen:
+            y, z = terms(bra, ket, place[q], w, w_sum)
+            for k in range(kind_count):
+                sums[l][k] = sums[l][k] + shares[l][q][k] * (z if k == kind_count - 1 else y)
+
+    def turn(state, l, chosen, place):
+        for q in chosen:
+            state = gate(state, place[q], coefs[l][q])
+        return state
+
+    def prepare(buffer, sign):
+        ket = (buffer[:, 0] * sign, buffer[:, 1] * sign)
+        weight = scale * buffer[:, 2]
+        return ket, (weight * ket[0], weight * ket[1])
+
+    def times(state, sign):
+        return (state[0] * sign, state[1] * sign)
+
+    every = range(qubits)
+    moved = [q for q in every if away[q][0] == DEVICE]
+    first, last = min(moved), max(moved)
+    late_edges = [q for q in every if first - 1 <= q <= last]
+    early_edges = [q for q in every if q not in late_edges]
+    local = [q for q in every if home[q][0] != DEVICE]
+    outer = [q for q in every if home[q][0] == DEVICE]
+
+    sign = edge_sign(home, qubits, every, majors, me)
+    ket, bra = prepare(sent1, sign)
+    add_terms(1, local, home, bra, ket)
+    ket, bra = (times(turn(x, 1, local, home), sign) for x in (ket, bra))
+    add_terms(0, local[1:-1], home, bra, ket)
+
+    sign = edge_sign(away, qubits, every, majors, me)
+    early = edge_sign(away, qubits, early_edges, majors, me)
+    arrive1()
+    ket, bra = prepare(held1, sign)
+    here = [q for q in every if away[q][0] != DEVICE]
+    bra_mid = times(turn(bra, 1, here, away), early)
+    ready = [q for q in here if q not in (first - 1, last + 1)]
+    done = turn(bra_mid, 0, ready, away)
+    sent2[:, 0] = done[0]
+    sent2[:, 1] = done[1]
+    start2()
+    held2[me] = sent2[me]
+    add_terms(1, outer, away, bra, ket)
+    ket = times(turn(ket, 1, here, away), early)
+    add_terms(0, [local[-1]] + outer + [0], away, bra_mid, ket)
+
+    at = [lax.broadcasted_iota(jnp.int32, (layers, 128), d) for d in range(2)]
+    total = jnp.zeros((layers, 128), jnp.float32)
+    for l in range(layers):
+        for k in range(kind_count):
+            total = total + jnp.where((at[0] == l) & (at[1] == k), jnp.sum(sums[l][k]), 0.0)
+    gsent[...] = total
+    gstart()
+    gheld[me] = total
+
+    late = edge_sign(home, qubits, late_edges, majors, me)
+    arrive2()
+    bra = (held2[:, 0], held2[:, 1])
+    bra = times(turn(bra, 1, moved, home), late)
+    bra = turn(bra, 0, [q for q in local if q not in ready], home)
+    for part, value in enumerate(bra):
+        for bit in (1, 2):
+            value = swap_bits(value, major_bits - 3 + bit, bit)
+        out_ref[pl.ds(part, rows, stride=2), :] = value.reshape(rows, 128)
+    garrive()
+    grads_ref[...] = jnp.sum(gheld[...], axis=0)
+    depart1()
+    depart2()
+    gdepart()
+
+
+def by_exchange(ket_state, observable, angles, gate_kinds):
+    amp_count = ket_state.shape[1]
+    n = lax.axis_size("amp")
+    qubits = (amp_count * n).bit_length() - 1
+    layers, kind_count = angles.shape
+    rows = amp_count // 128
+    ket = ket_state.reshape(2, rows, 128).transpose(1, 0, 2).reshape(2 * rows, 128)
+    vmem = pl.BlockSpec(memory_space=pltpu.VMEM)
+    smem = pl.BlockSpec(memory_space=pltpu.SMEM)
+    f32 = jnp.float32
+    out, grads = pl.pallas_call(
+        functools.partial(kernel, n, qubits),
+        out_shape=(
+            jax.ShapeDtypeStruct((2 * rows, 128), f32),
+            jax.ShapeDtypeStruct((layers, 128), f32),
+        ),
+        in_specs=[smem, smem, vmem, vmem],
+        out_specs=(vmem, vmem),
+        scratch_shapes=[
+            pltpu.VMEM((n, 3, 8, 128), f32),
+            pltpu.VMEM((n, 3, 8, 128), f32),
+            pltpu.VMEM((n, 2, 8, 128), f32),
+            pltpu.VMEM((n, 2, 8, 128), f32),
+            pltpu.VMEM((layers, 128), f32),
+            pltpu.VMEM((n, layers, 128), f32),
+        ]
+        + [pltpu.SemaphoreType.DMA((n,))] * 6,
+        compiler_params=pltpu.CompilerParams(collective_id=0, has_side_effects=True),
+    )(angles, gate_kinds, ket, observable.reshape(rows, 128))
+    bra_state = out.reshape(rows, 2, 128).transpose(1, 0, 2).reshape(2, amp_count)
+    return (bra_state, grads[:, :kind_count])
+
+
+def per_device(ket_state, observable, angles, gate_kinds):
+    tiles = ket_state.shape[1] // (1 << LANE_BITS + SUB_BITS)
+    if tiles == lax.axis_size("amp") and tiles >= 8 and angles.shape == (2, 3):
+        return by_exchange(ket_state, observable, angles, gate_kinds)
+    return on_device(ket_state, observable, angles, gate_kinds)
+
+
 def solution(mesh):
     placed = (P(None, "amp"), P("amp"), P(), P())
     return jax.shard_map(
-        on_device, mesh=mesh, in_specs=placed, out_specs=(P(None, "amp"), P()), check_vma=False
+        per_device, mesh=mesh, in_specs=placed, out_specs=(P(None, "amp"), P()), check_vma=False
     )

time: 366 us -> 36.3 us (0.10)
  other arithmetic: 100 us -> 0 us
  between operations: 79.5 us -> 0.65 us
  waiting for transfers between devices: 56.3 us -> 0 us
  blocking collectives: 39.6 us -> 0 us
  Pallas kernels: 0 us -> 33.3 us
  loops' own time: 30.8 us -> 0 us
  local copies, waits for them, and re-layouts: 29 us -> 2.24 us
  starting transfers between devices: 20.4 us -> 0 us
  matrix products: 8.27 us -> 0 us
    ppermute x20 -> x0, waiting for transfers between devices: 56.3 us -> none  [from_partner(): return lax.ppermute(value, axis, pairs)]
    reduce_sum x23 -> x0, other arithmetic: 47.8 us -> none  [the longest x6 29.1 us: rotation_of(): rotation = jnp.sum(jnp.where(chosen, angles[layer_id], 0.0))]
    psum x1 -> x0, blocking collectives: 39.6 us -> none  [on_device(): grads = lax.psum(grads_local, 'amp')]
    add x20 -> x0, other arithmetic: 35.6 us -> none  [the longest x2 25.1 us: on_device(): layer_terms = layer_terms + partial_value]
    pallas_call x0 -> x1, Pallas kernels: none -> 33.3 us  [by_exchange(): pl.pallas_call(functools.partial(kernel, n, qubits), out_shape=(jax.Shape...]
    another operation x26 -> x0, loops' own time: 30.8 us -> none  [the longest x16 30.3 us: rotate_position(): lax.cond(kind_id == 2, turn_z, turn_y, (ket_state.reshape(fold_shape), br...]
    ppermute x20 -> x0, starting transfers between devices: 20.4 us -> none  [from_partner(): return lax.ppermute(value, axis, pairs)]
    another operation x86 -> x0, local copies, waits for them, and re-layouts: 18.7 us -> none
  transfers between devices with their start and end apart: 20 -> 0, of which waited for: 13 -> 0; matrix products, arithmetic and copies ran while one was open for 8% -> 0% of each run, Pallas kernels for 0% -> 0%
where the time goes in v1:
time: 36.3 us; the launch traced here: 36.2 us
  Pallas kernels  33.3 us (92%)
  local copies, waits for them, and re-layouts  2.24 us (6%)
  between operations  0.65 us (2%)
    pallas_call x1, Pallas kernels, by_exchange(): pl.pallas_call(functools.partial(kernel, n, qubits), out_shape=(jax.Shape...  33.3 us
    unnamed x4, local copies, waits for them, and re-layouts  2.24 us

profile of v1, /device:TPU:0, one launch (start us, length us, event | category | flops | bytes accessed | tf_op | source)
XLA Modules:
  0.0 36.2 jit_solution(15337087533010929371)
XLA Ops:
  0.6 33.3 %shard_map.59 = (f32[512,128]{1,0:T(8,128)}, f32[2,128]{1,0:T(2,128)}) custom-call(f32[2,3]{1,0:T(2,128)} %angles.1, s32[2,32]{1,0:T(2,128)} %kinds.1, f32[512,128]{1,0:T(8,128)} %bitcast.12, f32[256,128]{1,0:T(8,128)} %bitcast.14), custom_call_target="tpu_custom_call" | custom-call | tf_op jit(solution)/shard_map/pallas_call | solution.py:567
  33.9 0.0 copy-start
  34.0 1.7 %copy.10 = f32[2,32768]{1,0:T(2,128)} copy(f32[2,32768]{1,0:T(2,128)} %bitcast.13) | data formatting | bytes 524288
  35.6 0.0 copy-done
  35.6 0.6 %copy.11 = f32[2,3]{1,0:T(2,128)} copy(f32[2,3]{1,0:T(2,128)S(1)} %bitcast.15) | data formatting | bytes 48
Async XLA Ops:
  33.9 1.7 %copy-start = (f32[2,128]{1,0:T(2,128)S(1)}, f32[2,128]{1,0:T(2,128)}, u32[]{:S(2)}) copy-start(f32[2,128]{1,0:T(2,128)} %get-tuple-element.5) | copy-start | bytes 3076

commit v2 on v1

--- a/solution.py
+++ b/solution.py
@@ -355,6 +355,30 @@
     )
 
 
+def lane_matrix(coefs):
+    at = [lax.broadcasted_iota(jnp.int32, (128, 128), d) for d in range(2)]
+    re, im = None, None
+    for bit, (c, sy, sz) in enumerate(coefs):
+        old, new = (x >> bit & 1 for x in at)
+        z = (1 - 2 * new).astype(jnp.float32)
+        same = old == new
+        a, b = jnp.where(same, c, sy * z), jnp.where(same, sz * z, 0.0)
+        re, im = (a, b) if re is None else (re * a - im * b, re * b + im * a)
+    return jnp.concatenate([jnp.concatenate([re, im], 1), jnp.concatenate([-im, re], 1)], 0)
+
+
+def turn_lanes(state, matrix):
+    re, im = (x.reshape(-1, 128) for x in state)
+    both = lax.dot_general(
+        jnp.concatenate([re, im], axis=1),
+        matrix[...],
+        (((1,), (0,)), ((), ())),
+        precision=lax.Precision.HIGH,
+        preferred_element_type=jnp.float32,
+    )
+    return both[:, :128].reshape(state[0].shape), both[:, 128:].reshape(state[0].shape)
+
+
 def terms(bra, ket, place, w, w_sum):
     axis, bit = place
     if axis == MAJOR:
@@ -397,8 +421,8 @@
 
 def kernel(
     n, qubits, angles, kinds, ket_ref, obs_ref, out_ref, grads_ref,
-    sent1, held1, sent2, held2, gsent, gheld,
-    send1, recv1, send2, recv2, gsend, grecv,
+    ket_in, obs_in, sent1, held1, sent2, held2, gsent, gheld, gsent2, gheld2,
+    send1, recv1, send2, recv2, gsend, grecv, gsend2, grecv2, load, wide,
 ):
     me = lax.axis_index("amp")
     majors = n
@@ -407,17 +431,31 @@
     home, away = layouts(major_bits, qubits - local_bits)
     scale = 2.0 / math.sqrt(2**qubits)
 
+    loads = [
+        pltpu.make_async_copy(ket_ref, ket_in, load.at[0]),
+        pltpu.make_async_copy(obs_ref, obs_in, load.at[1]),
+    ]
+    for copy in loads:
+        copy.start()
+
+    half = n // 2
+    high, low = me // half, me % half
+
+    def peer(k, sign):
+        side = (high + 1 - k // half) % 2
+        return side * half + (low + half + sign * (k % half)) % half
+
     barrier = pltpu.get_barrier_semaphore()
-
-    @pl.loop(1, n)
-    def _(k):
-        pl.semaphore_signal(barrier, inc=1, device_id=((me + k) % n,), device_id_type=MESH)
+    for k in [k for k in range(n) if k != half]:
+        pl.semaphore_signal(barrier, inc=1, device_id=(peer(k, 1),), device_id_type=MESH)
+    for copy in loads:
+        copy.wait()
 
     rows = 8 * majors
     raw = [
-        ket_ref[pl.ds(0, rows, stride=2), :],
-        ket_ref[pl.ds(1, rows, stride=2), :],
-        obs_ref[...],
+        ket_in[pl.ds(0, rows, stride=2), :],
+        ket_in[pl.ds(1, rows, stride=2), :],
+        obs_in[...],
     ]
     for part, value in enumerate(raw):
         value = value.reshape(majors, 8, 128)
@@ -427,37 +465,53 @@
 
     pl.semaphore_wait(barrier, n - 1)
 
-    def exchange(source, target, send, recv, whole):
+    def exchange(source, target, send, recv):
         def copy(k, block, slot):
             return pltpu.make_async_remote_copy(
-                src_ref=source if whole else source.at[block],
+                src_ref=source.at[block],
                 dst_ref=target.at[slot],
                 send_sem=send.at[k],
                 recv_sem=recv.at[k],
-                device_id=((me + k) % n,),
+                device_id=(peer(k, 1),),
                 device_id_type=MESH,
             )
 
+        def each(act):
+            for lower, upper in ((0, half), (half + 1, n)):
+                pl.loop(lower, upper)(act)
+
         def start():
-            @pl.loop(1, n)
-            def _(k):
-                copy(k, (me + k) % n, me).start()
+            each(lambda k: copy(k, peer(k, 1), me).start())
 
         def arrive():
-            @pl.loop(1, n)
-            def _(k):
-                copy(k, (me + k) % n, (me + n - k) % n).wait_recv()
+            each(lambda k: copy(k, peer(k, 1), peer(k, -1)).wait_recv())
 
         def depart():
-            @pl.loop(1, n)
-            def _(k):
-                copy(k, (me + k) % n, me).wait_send()
+            each(lambda k: copy(k, peer(k, 1), me).wait_send())
 
         return start, arrive, depart
 
-    start1, arrive1, depart1 = exchange(sent1, held1, send1, recv1, False)
-    start2, arrive2, depart2 = exchange(sent2, held2, send2, recv2, False)
-    gstart, garrive, gdepart = exchange(gsent, gheld, gsend, grecv, True)
+    def gather(source, target, send, recv, stride, count):
+        digit = me // stride % count
+
+        def copies():
+            for k in range(1, count):
+                yield pltpu.make_async_remote_copy(
+                    src_ref=source,
+                    dst_ref=target.at[k],
+                    send_sem=send.at[k],
+                    recv_sem=recv.at[k],
+                    device_id=(me + ((digit + k) % count - digit) * stride,),
+                    device_id_type=MESH,
+                )
+
+        target[0] = source[...]
+        for copy in copies():
+            copy.start()
+        return lambda: [copy.wait_recv() for copy in copies()], lambda: [copy.wait_send() for copy in copies()]
+
+    start1, arrive1, depart1 = exchange(sent1, held1, send1, recv1)
+    start2, arrive2, depart2 = exchange(sent2, held2, send2, recv2)
     start1()
     held1[me] = sent1[me]
 
@@ -476,6 +530,10 @@
         coefs.append(row)
         shares.append(share)
 
+    for l in range(layers):
+        wide[l] = lane_matrix(coefs[l][:LANE_BITS])
+    matrices = [wide.at[l] for l in range(layers)]
+
     sums = [[jnp.zeros((8, 128), jnp.float32) for _ in range(kind_count)] for _ in range(layers)]
 
     def add_terms(l, chosen, place, bra, ket):
@@ -487,6 +545,10 @@
                 sums[l][k] = sums[l][k] + shares[l][q][k] * (z if k == kind_count - 1 else y)
 
     def turn(state, l, chosen, place):
+        lanes = set(range(LANE_BITS))
+        if lanes <= set(chosen):
+            state = turn_lanes(state, matrices[l])
+            chosen = [q for q in chosen if q not in lanes]
         for q in chosen:
             state = gate(state, place[q], coefs[l][q])
         return state
@@ -534,9 +596,12 @@
     for l in range(layers):
         for k in range(kind_count):
             total = total + jnp.where((at[0] == l) & (at[1] == k), jnp.sum(sums[l][k]), 0.0)
+    inner = gheld.shape[0]
     gsent[...] = total
-    gstart()
-    gheld[me] = total
+    garrive, gdepart = gather(gsent, gheld, gsend, grecv, 1, inner)
+    garrive()
+    gsent2[...] = jnp.sum(gheld[...], axis=0)
+    garrive2, gdepart2 = gather(gsent2, gheld2, gsend2, grecv2, inner, n // inner)
 
     late = edge_sign(home, qubits, late_edges, majors, me)
     arrive2()
@@ -547,11 +612,12 @@
         for bit in (1, 2):
             value = swap_bits(value, major_bits - 3 + bit, bit)
         out_ref[pl.ds(part, rows, stride=2), :] = value.reshape(rows, 128)
-    garrive()
-    grads_ref[...] = jnp.sum(gheld[...], axis=0)
+    garrive2()
+    grads_ref[...] = jnp.sum(gheld2[...], axis=0)
     depart1()
     depart2()
     gdepart()
+    gdepart2()
 
 
 def by_exchange(ket_state, observable, angles, gate_kinds):
@@ -563,6 +629,9 @@
     ket = ket_state.reshape(2, rows, 128).transpose(1, 0, 2).reshape(2 * rows, 128)
     vmem = pl.BlockSpec(memory_space=pltpu.VMEM)
     smem = pl.BlockSpec(memory_space=pltpu.SMEM)
+    hbm = pl.BlockSpec(memory_space=pl.ANY)
+    inner = 1 << n.bit_length() // 2
+    outer = n // inner
     f32 = jnp.float32
     out, grads = pl.pallas_call(
         functools.partial(kernel, n, qubits),
@@ -570,17 +639,22 @@
             jax.ShapeDtypeStruct((2 * rows, 128), f32),
             jax.ShapeDtypeStruct((layers, 128), f32),
         ),
-        in_specs=[smem, smem, vmem, vmem],
+        in_specs=[smem, smem, hbm, hbm],
         out_specs=(vmem, vmem),
         scratch_shapes=[
+            pltpu.VMEM((2 * rows, 128), f32),
+            pltpu.VMEM((rows, 128), f32),
             pltpu.VMEM((n, 3, 8, 128), f32),
             pltpu.VMEM((n, 3, 8, 128), f32),
             pltpu.VMEM((n, 2, 8, 128), f32),
             pltpu.VMEM((n, 2, 8, 128), f32),
             pltpu.VMEM((layers, 128), f32),
-            pltpu.VMEM((n, layers, 128), f32),
+            pltpu.VMEM((inner, layers, 128), f32),
+            pltpu.VMEM((layers, 128), f32),
+            pltpu.VMEM((outer, layers, 128), f32),
         ]
-        + [pltpu.SemaphoreType.DMA((n,))] * 6,
+        + [pltpu.SemaphoreType.DMA((size,)) for size in (n, n, n, n, inner, inner, outer, outer, 2)]
+        + [pltpu.VMEM((layers, 256, 256), f32)],
         compiler_params=pltpu.CompilerParams(collective_id=0, has_side_effects=True),
     )(angles, gate_kinds, ket, observable.reshape(rows, 128))
     bra_state = out.reshape(rows, 2, 128).transpose(1, 0, 2).reshape(2, amp_count)

time: 36.3 us -> 33.6 us (0.926)
  Pallas kernels: 33.3 us -> 30.6 us
    pallas_call x1, Pallas kernels: 33.3 us -> 30.6 us  [by_exchange(): pl.pallas_call(functools.partial(kernel, n, qubits), out_shape=(jax.Shape...]
where the time goes in v2:
time: 33.6 us; the launch traced here: 33.5 us
  Pallas kernels  30.6 us (91%)
  local copies, waits for them, and re-layouts  2.24 us (7%)
  between operations  0.65 us (2%)
    pallas_call x1, Pallas kernels, by_exchange(): pl.pallas_call(functools.partial(kernel, n, qubits), out_shape=(jax.Shape...  30.6 us
    unnamed x4, local copies, waits for them, and re-layouts  2.24 us

profile of v2, /device:TPU:0, one launch (start us, length us, event | category | flops | bytes accessed | tf_op | source)
XLA Modules:
  0.0 33.5 jit_solution(17684440150257242487)
XLA Ops:
  0.6 30.6 %shard_map.59 = (f32[512,128]{1,0:T(8,128)}, f32[2,128]{1,0:T(2,128)}) custom-call(f32[2,3]{1,0:T(2,128)} %angles.1, s32[2,32]{1,0:T(2,128)} %kinds.1, f32[512,128]{1,0:T(8,128)} %bitcast.12, f32[256,128]{1,0:T(8,128)} %bitcast.14), custom_call_target="tpu_custom_call" | custom-call | tf_op jit(solution)/shard_map/pallas_call | solution.py:636
  31.2 0.0 copy-start
  31.2 1.7 %copy.10 = f32[2,32768]{1,0:T(2,128)} copy(f32[2,32768]{1,0:T(2,128)} %bitcast.13) | data formatting | bytes 524288
  32.9 0.0 copy-done
  32.9 0.6 %copy.11 = f32[2,3]{1,0:T(2,128)} copy(f32[2,3]{1,0:T(2,128)S(1)} %bitcast.15) | data formatting | bytes 48
Async XLA Ops:
  31.2 1.7 %copy-start = (f32[2,128]{1,0:T(2,128)S(1)}, f32[2,128]{1,0:T(2,128)}, u32[]{:S(2)}) copy-start(f32[2,128]{1,0:T(2,128)} %get-tuple-element.5) | copy-start | bytes 3076
